TPU v7x, 32 devices: a whole 2x2x4 slice. The times are simulated.
32 devices in a mesh: freq: 8 (over y, x, core), base: 4 (over z).
Axes of the slice: x: 2, y: 2, z: 4, core: 2. Of those that a mesh axis runs over, the one named last changes fastest.
Arguments:
- visibility: float32 [2, 16, 2048], P(None, 'freq', 'base'), may hold values from -6 to 6
- tile_of: int32 [16, 2048, 1], P('freq', 'base'), may hold values from 0 to 3; in each aligned block of 512 rows (0 to 511, 512 to 1023, ..., all dimensions but the last counted through in order) at most 256 rows name the same one
- u_within: int32 [16, 2048], P('freq', 'base'), may hold values from 0 to 255
- v_cell: int32 [16, 2048], P('freq', 'base'), may hold values from 0 to 1016
- kernel_index: int32 [2, 16, 2048], P(None, 'freq', 'base'), may hold values from 0 to 127
- kernel: float32 [128, 8], replicated, may hold values from 0.1 to 1
- live_count: int32 [16, 4], P('freq', 'base'), may hold values from 64 to 512, as said below
- bin_map: int32 [1024, 1024], P('base'), may hold values from 0 to 511, as said below
Outputs:
- power_map: float32 [1024, 1024], P('freq', 'base')
- spectrum: float32 [512], replicated
Inputs may be any that keep to these rules, and one draw needn't show every extreme that they name: `tile_of`: among the visibilities of one channel on one device, at most 256 name the same tile, and in some device's visibilities a tile is named by exactly 256. `live_count`: the first device along base holds 512 used slots in every channel; the used slots of a device are its first ones. `bin_map`: every bin number occurs.
All inputs are finite; a program needn't handle non-finite values.
Results may differ from a plain program's by a relative error of at most 0.0003.
Values sent between devices are 32-bit elements; how exact they have to be, the bound alone decides.
A program may use at most 128 MiB of HBM per device.

v0:
```python
import math
import jax
import jax.numpy as jnp
from jax import lax
from jax.sharding import PartitionSpec as P

G = 1024
NBINS = 512
KW = 8
HIGHEST_PRECISION = lax.Precision.HIGHEST


def passed_along(x, axis, by):
    peers = lax.axis_size(axis)
    pairs = [(i, i + by) for i in range(peers) if 0 <= i + by < peers]
    return lax.ppermute(x, axis, pairs)


def look_up_taps(kernel_index, kernel):
    table_rows = kernel.shape[0]
    onehot = (kernel_index[..., None] == jnp.arange(table_rows, dtype=jnp.int32)).astype(
        jnp.float32
    )
    return jnp.einsum("acno,ot->actn", onehot, kernel, precision=HIGHEST_PRECISION)


def visibility_fields(
    visibility, tile_of, u_within, v_cell, kernel_index, kernel, live_count, tile_rows
):
    slots = u_within.shape[1]
    is_live = jnp.arange(slots, dtype=jnp.int32)[None, :] < live_count
    zeroed = jnp.zeros_like(visibility[0])
    real_part = jnp.where(is_live, visibility[0], zeroed)
    imag_part = jnp.where(is_live, visibility[1], zeroed)
    tile_index = tile_of[:, :, 0]
    u_cell = jnp.minimum(tile_index * tile_rows + u_within, G - KW)
    u_cell = u_cell - tile_index * tile_rows
    taps = look_up_taps(kernel_index, kernel)
    fields = jnp.concatenate(
        [
            real_part[:, None],
            imag_part[:, None],
            u_cell[:, None].astype(jnp.float32),
            v_cell[:, None].astype(jnp.float32),
            taps[0],
            taps[1],
        ],
        axis=1,
    )
    return (fields, is_live, tile_index)


def row_taps(fields, row_start, row_count):
    u_cell = fields[2].astype(jnp.int32)
    offset = row_start + jnp.arange(row_count, dtype=jnp.int32)[None, :] - u_cell[:, None]
    taps = jnp.zeros(offset.shape, jnp.float32)
    for tap_index in range(KW):
        taps = taps + jnp.where(offset == tap_index, fields[4 + tap_index][:, None], 0.0)
    return taps


def column_side(fields):
    v_start = fields[3].astype(jnp.int32)
    offset = jnp.arange(G, dtype=jnp.int32)[None, :] - v_start[:, None]
    taps = jnp.zeros(offset.shape, jnp.float32)
    for tap_index in range(KW):
        taps = taps + jnp.where(offset == tap_index, fields[4 + KW + tap_index][:, None], 0.0)
    return jnp.concatenate([fields[0][:, None] * taps, fields[1][:, None] * taps], axis=1)


def contract_slots(upper, lower):
    return lax.dot_general(upper, lower, (((0,), (0,)), ((), ())), precision=HIGHEST_PRECISION)


def grid_rows(fields, row_start, row_count):
    return contract_slots(row_taps(fields, row_start, row_count), column_side(fields))


def dft_matrix():
    positions = jnp.arange(G, dtype=jnp.int32)
    phase = positions[:, None] * positions[None, :] % G
    angle = phase.astype(jnp.float32) * (2.0 * math.pi / G)
    cosine = jnp.cos(angle)
    sine = jnp.sin(angle)
    return jnp.concatenate(
        [jnp.concatenate([cosine, -sine], axis=1), jnp.concatenate([sine, cosine], axis=1)], axis=0
    )


def row_transform(grid_tile, dft_table, tile_rows, channels_here):
    flat_rows = grid_tile.reshape(tile_rows * channels_here, 2 * G)
    halves = jnp.stack(
        [
            jnp.dot(flat_rows, dft_table[:, :G], precision=HIGHEST_PRECISION),
            jnp.dot(flat_rows, dft_table[:, G:], precision=HIGHEST_PRECISION),
        ]
    )
    return halves.reshape(2, tile_rows, channels_here, G)


def to_columns(columns, tile_rows, channels_here):
    return columns.reshape(2 * G, channels_here * tile_rows)


def histogram(stacked, bins):
    row_total = bins.shape[0]
    block_rows = min(64, row_total)
    block_count = row_total // block_rows
    columns = bins.shape[1]
    value_blocks = stacked.reshape(2, block_count, block_rows * columns).transpose(1, 0, 2)
    bin_blocks = bins.reshape(block_count, block_rows * columns)

    def add_block(running, pieces):
        values, bin_ids = pieces
        onehot = (bin_ids[:, None] == jnp.arange(NBINS, dtype=jnp.int32)[None, :]).astype(
            jnp.float32
        )
        return (running + jnp.dot(values, onehot, precision=HIGHEST_PRECISION), None)

    result, _ = lax.scan(add_block, jnp.zeros((2, NBINS), jnp.float32), (value_blocks, bin_blocks))
    return result


def per_device(visibility, tile_of, u_within, v_cell, kernel_index, kernel, live_count, bin_map):
    base_count = lax.axis_size("base")
    freq_count = lax.axis_size("freq")
    tile_rows = G // base_count
    channels_here = visibility.shape[1]
    slots = visibility.shape[2]
    dft_table = dft_matrix()
    fields, is_live, tile_index = visibility_fields(
        visibility, tile_of, u_within, v_cell, kernel_index, kernel, live_count, tile_rows
    )
    capacity = 2 * slots // base_count
    field_count = fields.shape[1]
    chosen = (
        (tile_index[:, :, None] == jnp.arange(base_count, dtype=jnp.int32)[None, None, :])
        & is_live[:, :, None]
    ).astype(jnp.int32)
    before_count = jnp.sum((jnp.cumsum(chosen, axis=1) - chosen) * chosen, axis=2)
    target = jnp.where(is_live, tile_index * capacity + before_count, base_count * capacity)
    outgoing = []
    for channel in range(channels_here):
        placed = (
            jnp.zeros((base_count * capacity, field_count), jnp.float32)
            .at[target[channel]]
            .set(fields[channel].T, mode="drop")
        )
        outgoing.append(placed.reshape(base_count, capacity, field_count).transpose(0, 2, 1))
    received = lax.all_to_all(
        jnp.stack(outgoing, axis=1), "base", split_axis=0, concat_axis=0, tiled=True
    )
    extended = []
    for channel in range(channels_here):
        slot_fields = (
            received[:, channel].transpose(1, 0, 2).reshape(field_count, base_count * capacity)
        )
        extended.append(grid_rows(slot_fields, 0, tile_rows + KW).reshape(tile_rows + KW, 2, G))
    extended = jnp.stack(extended, axis=1)
    incoming = passed_along(extended[tile_rows:], "base", 1)
    grid_tile = extended[:tile_rows].at[:KW].add(incoming)
    halves = row_transform(grid_tile, dft_table, tile_rows, channels_here)
    columns = lax.all_to_all(halves, "base", split_axis=3, concat_axis=1, tiled=True)
    stacked = to_columns(columns, tile_rows, channels_here)
    spectra = contract_slots(dft_table, stacked)
    normalizer = 1.0 / (channels_here * freq_count * slots * base_count)
    squared = spectra[:G] * spectra[:G] + spectra[G:] * spectra[G:]
    power_part = jnp.sum(squared.reshape(G, channels_here, tile_rows), axis=1) * normalizer
    bins_here = bin_map.T
    share_rows = G // freq_count
    share_start = lax.axis_index("freq") * share_rows
    power_share = lax.psum_scatter(power_part, "freq", scatter_dimension=0, tiled=True)
    bins_share = lax.dynamic_slice_in_dim(bins_here, share_start, share_rows, 0)
    bin_sums_local = histogram(jnp.stack([power_share, jnp.ones_like(power_share)]), bins_share)
    totals, counts = lax.psum((bin_sums_local[0], bin_sums_local[1]), ("freq", "base"))
    return (power_share, totals / counts)


def solution(mesh):
    in_specs = (
        P(None, "freq", "base"),
        P("freq", "base", None),
        P("freq", "base"),
        P("freq", "base"),
        P(None, "freq", "base"),
        P(),
        P("freq", "base"),
        P("base", None),
    )
    out_specs = (P("freq", "base"), P())
    return jax.shard_map(
        per_device, mesh=mesh, in_specs=in_specs, out_specs=out_specs, check_vma=False
    )
```

profile of v0, /device:TPU:0, one launch (start us, length us, event | category | flops | bytes accessed | tf_op | source)
XLA Modules:
  0.0 432.0 jit_solution(2849988539622279299)
XLA Ops:
  7.2 0.8 iota_compare_fusion.8
  8.0 0.7 broadcast_compare_fusion
  8.7 0.7 copy.136
  9.4 0.7 fusion.149
  10.1 2.4 reduce-window.6
  13.3 0.8 subtract_convert_fusion
  14.1 0.7 fusion.177
  14.8 1.6 convolution_bitcast_fusion
  16.4 0.7 convert_element_type.75
  17.1 0.7 compare_select_fusion.2
  18.3 1.8 scatter_custom_fusion
  20.5 1.8 scatter_custom_fusion.1
  22.6 0.8 copy.65
  23.4 6.3 %all-to-all-start = ((f32[4,2,20,256]{3,1,2,0:T(2,128)}), f32[4,2,20,256]{3,1,2,0:T(2,128)S(1)}, u32[]{:S(2)}, u32[]{:S(2)}) async-start(f32[4,2,20,256]{3,1,2,0:T(2,128)} %copy.65), calls=%async_computation | async-start | bytes 327680 | tf_op jit(solution)/shard_map/all_to_all | solution.py:150
  29.7 17.5 %fusion.36 = (f32[1024,1024]{1,0:T(8,128)}, f32[1024,1024]{1,0:T(8,128)}) fusion(), kind=kLoop, calls=%fused_computation.59 | loop fusion | flops 14680064 | bytes 8388608 | tf_op jit(solution)/shard_map/sin | solution.py:84
  47.3 16.5 %fusion.38 = f32[1024,1024]{1,0:T(8,128)} fusion(), kind=kLoop, calls=%fused_computation.61 | loop fusion | flops 15728640 | bytes 4194304 | tf_op jit(solution)/shard_map/neg | solution.py:86
  64.2 4.4 %broadcast_multiply_fusion.1 = (f32[1024,1024]{1,0:T(8,128)S(1)}, f32[1024,1024]{1,0:T(8,128)S(1)}) fusion(f32[1024]{0:T(1024)S(1)} %bitcast.240, f32[1024]{0:T(1024)S(1)} %bitcast.258, f32[1024]{0:T(1024)S(1)} %bitcast.256, f32[1024]{0:T(1024)S(1)} %bitcast.254, f32[1024]{0:T(1024)S(1)} %bitcast.252, f32[1024]{0:T(1024)S(1)} %bitcast.250, ...), kind=kLoop, calls=%fused_computation.56 | loop fusion | flops 27262976 | bytes 8433664 | tf_op jit(solution)/shard_map/mul | solution.py:68
  68.6 10.1 %fusion.9 = f32[264,2048]{1,0:T(8,128)} fusion(f32[1024,1024]{1,0:T(8,128)S(1)} %get-tuple-element.127, f32[1024,1024]{1,0:T(8,128)S(1)} %get-tuple-element.126, f32[1024]{0:T(1024)S(1)} %bitcast.276, f32[1024]{0:T(1024)S(1)} %bitcast.274, f32[1024]{0:T(1024)S(1)} %bitcast.272, f32[1024]{0:T(1024)S(1)} %bitcast.270, f32[1024]{0:T(1024)S(1)} %bitcast.284, ...), kind=kOutput, calls=%fused_computation.18 | convolution fusion | flops 6652362752 | bytes 10588160 | tf_op jit(solution)/shard_map/dot_general | solution.py:72
  78.7 3.2 stack_reshape.7
  82.1 4.1 broadcast_multiply_fusion.3
  86.2 10.1 %fusion.5 = f32[264,2048]{1,0:T(8,128)} fusion(f32[1024,1024]{1,0:T(8,128)S(1)} %get-tuple-element.129, f32[1024,1024]{1,0:T(8,128)S(1)} %get-tuple-element.128, f32[1024]{0:T(1024)S(1)} %bitcast.285, f32[1024]{0:T(1024)S(1)} %bitcast.283, f32[1024]{0:T(1024)S(1)} %bitcast.281, f32[1024]{0:T(1024)S(1)} %bitcast.279, f32[1024]{0:T(1024)S(1)} %bitcast.277, ...), kind=kOutput, calls=%fused_computation.14 | convolution fusion | flops 6652362752 | bytes 10588160 | tf_op jit(solution)/shard_map/dot_general | solution.py:72
  96.3 4.1 stack_reshape.6
  100.4 2.5 constant_dynamic-update-slice_fusion.1
  102.9 0.9 constant_dynamic-update-slice_fusion
  103.8 3.9 collective-permute-start
  107.8 12.9 %maximum_maximum_fusion = f32[2048,2048]{1,0:T(8,128)} fusion(f32[1024,1024]{1,0:T(8,128)S(1)} %copy-done.3, f32[1024,1024]{1,0:T(8,128)S(1)} %copy-done.1, f32[1024,1024]{1,0:T(8,128)} %fusion.38), kind=kLoop, calls=%fused_computation.9 | loop fusion | flops 12582912 | bytes 29360128 | tf_op jit(solution)/shard_map/concatenate | solution.py:85
  120.7 3.4 slice.363
  124.1 0.7 fusion.144
  124.8 6.7 %reshape.405 = f32[256,2,2048]{2,0,1:T(8,128)} reshape(f32[256,2,2,1024]{3,2,0,1:T(2,128)} %fusion.144) | data formatting | bytes 8388608 | tf_op jit(solution)/shard_map/reshape.292
  131.5 16.9 %fusion.39 = f32[1,256,2,1024]{3,1,2,0:T(8,128)S(1)} fusion(f32[256,2,2048]{2,0,1:T(8,128)} %reshape.405, f32[2048,2048]{1,0:T(8,128)} %maximum_maximum_fusion), kind=kOutput, calls=%fused_computation.62 | convolution fusion | flops 12884901888 | bytes 14680064 | tf_op jit(solution)/shard_map/dot_general | solution.py:94
  148.4 16.3 %fusion.40 = f32[1,256,2,1024]{3,1,2,0:T(8,128)S(1)} fusion(f32[256,2,2048]{2,0,1:T(8,128)S(1)} %copy-done.5, f32[2048,2048]{1,0:T(8,128)} %maximum_maximum_fusion), kind=kOutput, calls=%fused_computation.63 | convolution fusion | flops 12884901888 | bytes 14680064 | tf_op jit(solution)/shard_map/dot_general | solution.py:95
  164.7 2.3 pad_maximum_fusion
  167.0 7.2 %copy.68 = f32[2,256,2,1024]{1,2,0,3:T(2,128)} copy(f32[2,256,2,1024]{3,1,2,0:T(8,128)} %pad_maximum_fusion) | data formatting | bytes 8388608 | tf_op jit(solution)/shard_map/stack | solution.py:92
  174.2 98.3 %all_to_all.20 = f32[2,256,2,1024]{1,2,0,3:T(2,128)} all-to-all(f32[2,256,2,1024]{1,2,0,3:T(2,128)} %copy.68), channel_id=1, replica_groups=mesh['freq'=8,'base'=4] {'base'}, dimensions={3} | all-to-all | bytes 8388608 | tf_op jit(solution)/shard_map/all_to_all | solution.py:163
  272.5 10.9 %copy.69 = f32[2,256,2,4,256]{4,2,1,3,0:T(2,128)} copy(f32[2,256,2,4,256]{1,2,0,4,3:T(2,128)} %bitcast.228) | data formatting | bytes 8388608 | tf_op jit(solution)/shard_map/all_to_all | solution.py:163
  283.4 4.9 %copy.120 = f32[256,8,2,256]{3,1,2,0:T(8,128)} copy(f32[256,8,2,256]{3,2,1,0:T(2,128)} %bitcast.229) | data formatting | bytes 8388608
  288.3 1.3 copy-done.4
  289.6 33.1 %fusion.175 = f32[2048,512]{0,1:T(8,128)S(1)} fusion(f32[2048,512]{1,0:T(8,128)} %bitcast.231, f32[1024,1024]{1,0:T(8,128)S(1)} %copy-done.4, f32[1024,1024]{1,0:T(8,128)S(1)} %copy-done.2, f32[1024,1024]{1,0:T(8,128)} %fusion.38), kind=kOutput, calls=%fused_computation.257 | convolution fusion | flops 25782386688 | bytes 20971520 | tf_op jit(solution)/shard_map/dot_general | solution.py:72
  323.2 1.2 reduce_sum.19
  324.4 2.3 broadcast_multiply_fusion.4
  327.0 34.9 %reduce-scatter.2.cloned.1.call-done = f32[128,256]{0,1:T(8,128)} async-done(((f32[1024,256]{0,1:T(8,128)}), f32[128,256]{0,1:T(8,128)}) %reduce-scatter.2.cloned.1.call-update) | async-done | bytes 131088 | tf_op jit(solution)/shard_map/reduce_scatter | solution.py:172
  361.9 1.0 copy.79
  363.1 21.1 %while.12 = (s32[]{:T(128)}, f32[2,512]{1,0:T(2,128)S(1)}, f32[2,2,16384]{2,0,1:T(2,128)S(1)}, s32[2,16384]{1,0:T(2,128)S(1)}, s32[]{:T(128)}, /*index=5*/s32[]{:T(128)}) while((s32[]{:T(128)}, f32[2,512]{1,0:T(2,128)S(1)}, f32[2,2,16384]{2,0,1:T(2,128)S(1)}, s32[2,16384]{1,0:T(2,128)S(1)}, s32[]{:T(128)}, ...), condition=%wide.region_8.9_spmd.clone, body=%wide.region_7.8_spmd.clone.sunk | while | flops 209717248 | bytes 598103 | solution.py:120
  363.4 10.3 %fusion.183 = f32[2,512]{1,0:T(2,128)S(1)} fusion(s32[16384]{0:T(1024)S(1)} %bitcast.235, f32[1,2,16384]{2,0,1:T(1,128)S(1)} %constant_dynamic-slice_fusion.5, f32[2,512]{1,0:T(2,128)S(1)} %get-tuple-element.176, pred[]{:T(512)S(6)} %compare.11), kind=kOutput, calls=%fused_computation.5.clone.1 | convolution fusion | flops 209717248 | bytes 204801 | tf_op jit(solution)/shard_map/while/body/eval_jaxpr/dot_general | solution.py:118
  373.9 10.3 %fusion.183 = f32[2,512]{1,0:T(2,128)S(1)} fusion(s32[16384]{0:T(1024)S(1)} %bitcast.235, f32[1,2,16384]{2,0,1:T(1,128)S(1)} %constant_dynamic-slice_fusion.5, f32[2,512]{1,0:T(2,128)S(1)} %get-tuple-element.176, pred[]{:T(512)S(6)} %compare.11), kind=kOutput, calls=%fused_computation.5.clone.1 | convolution fusion | flops 209717248 | bytes 204801 | tf_op jit(solution)/shard_map/while/body/eval_jaxpr/dot_general | solution.py:118
  384.2 39.3 %all-reduce.1 = (f32[512]{0:T(512)S(1)}, f32[512]{0:T(512)S(1)}) all-reduce(f32[512]{0:T(512)S(1)} %bitcast.265, f32[512]{0:T(512)S(1)} %bitcast.264), channel_id=1, replica_groups=mesh['freq'=8,'base'=4] {'freq','base'}, use_global_device_ids=true, to_apply=%region_9.10 | all-reduce | flops 1024 | bytes 8192 | tf_op jit(solution)/shard_map/psum | solution.py:175
  423.5 0.6 div.3
  424.1 0.8 copy.73
  (93 shorter events, 3.5 us)
Async XLA Ops:
  7.2 319.6 %copy-start = (s32[256,1024]{1,0:T(8,128)S(1)}, s32[256,1024]{1,0:T(8,128)}, u32[]{:S(2)}) copy-start(s32[256,1024]{1,0:T(8,128)} %param.19) | copy-start | bytes 3145732
  23.4 40.4 %all-to-all-start = ((f32[4,2,20,256]{3,1,2,0:T(2,128)}), f32[4,2,20,256]{3,1,2,0:T(2,128)S(1)}, u32[]{:S(2)}, u32[]{:S(2)}) async-start(f32[4,2,20,256]{3,1,2,0:T(2,128)} %copy.65), calls=%async_computation | async-start | bytes 327680 | tf_op jit(solution)/shard_map/all_to_all | solution.py:150
  29.7 332.2 %reduce-scatter.2.cloned.1.call-start = ((), (), s32[]{:S(2)}) async-start(), calls=%async_computation.3 | async-start | bytes 1179648 | tf_op jit(solution)/shard_map/reduce_scatter | solution.py:172
  100.4 7.4 %copy-start.1 = (f32[1024,1024]{1,0:T(8,128)S(1)}, f32[1024,1024]{1,0:T(8,128)}, u32[]{:S(2)}) copy-start(f32[1024,1024]{1,0:T(8,128)} %get-tuple-element.142) | copy-start | bytes 12582916
  100.4 7.4 %copy-start.3 = (f32[1024,1024]{1,0:T(8,128)S(1)}, f32[1024,1024]{1,0:T(8,128)}, u32[]{:S(2)}) copy-start(f32[1024,1024]{1,0:T(8,128)} %get-tuple-element.143) | copy-start | bytes 12582916
  103.8 20.3 %collective-permute-start = (f32[8,2,2,1024]{3,2,0,1:T(2,128)S(1)}, f32[8,2,2,1024]{3,2,0,1:T(2,128)S(1)}, u32[]{:S(2)}, u32[]{:S(2)}) collective-permute-start(f32[8,2,2,1024]{3,2,0,1:T(2,128)S(1)} %slice.365), channel_id=1, source_target_pairs={{0,1},{1,2},{2,3},{4,5},{5,6},{6,7},{8,9},{9,10},{10,11},{12,13},{... | collective-permute-start | bytes 393224 | tf_op jit(solution)/shard_map/ppermute | solution.py:16
  131.5 16.9 %copy-start.5 = (f32[256,2,2048]{2,0,1:T(8,128)S(1)}, f32[256,2,2048]{2,0,1:T(8,128)}, u32[]{:S(2)}) copy-start(f32[256,2,2048]{2,0,1:T(8,128)} %reshape.405) | copy-start | bytes 12582916
  283.4 4.9 %copy-start.2 = (f32[1024,1024]{1,0:T(8,128)S(1)}, f32[1024,1024]{1,0:T(8,128)}, u32[]{:S(2)}) copy-start(f32[1024,1024]{1,0:T(8,128)} %get-tuple-element.142) | copy-start | bytes 12582916
  283.4 6.2 %copy-start.4 = (f32[1024,1024]{1,0:T(8,128)S(1)}, f32[1024,1024]{1,0:T(8,128)}, u32[]{:S(2)}) copy-start(f32[1024,1024]{1,0:T(8,128)} %get-tuple-element.143) | copy-start | bytes 12582916
  363.1 61.0 %copy-start.6 = (f32[128,256]{0,1:T(8,128)S(1)}, f32[128,256]{0,1:T(8,128)}, u32[]{:S(2)}) copy-start(f32[128,256]{0,1:T(8,128)} %reduce-scatter.2.cloned.1.call-done) | copy-start | bytes 393220
Sparse Core Ops, SparseCore 0:
  326.8 35.0 reduce-scatter.1
where the time goes:
time: 440 us; the launch traced here: 432 us
  blocking collectives  138 us (31%)
  matrix products  109 us (25%)
  other arithmetic  70.4 us (16%)
  local copies, waits for them, and re-layouts  55.1 us (13%)
  waiting for transfers between devices  35 us (8%)
  between operations  14.9 us (3%)
  starting transfers between devices  10.3 us (2%)
    all_to_all x1, blocking collectives, per_device(): lax.all_to_all(halves, 'base', split_axis=3, concat_axis=1, tiled=True)  98.3 us
    dot_general x3, matrix products, contract_slots(): lax.dot_general(upper, lower, (((0,), (0,)), ((), ())), precision=HIGHEST...  53.3 us
    psum x1, blocking collectives, per_device(): lax.psum((bin_sums_local[0], bin_sums_local[1]), ('freq', 'base'))  39.3 us
    reduce_scatter x1, waiting for transfers between devices, per_device(): lax.psum_scatter(power_part, 'freq', scatter_dimension=0, tiled=True)  34.9 us
    dot_general x2, matrix products, add_block(): jnp.dot(values, onehot, precision=HIGHEST_PRECISION)  20.6 us
    sin x1, other arithmetic, dft_matrix(): sine = jnp.sin(angle)  17.5 us
    dot_general x1, matrix products, row_transform(): jnp.dot(flat_rows, dft_table[:, :G], precision=HIGHEST_PRECISION)  16.9 us
    neg x1, other arithmetic, dft_matrix(): -sine  16.5 us
  transfers between devices with their start and end apart: 3, of which 1 were waited for; matrix products, arithmetic and copies ran while one was open for 12% of the time, Pallas kernels for 0%

commit v1 on v0

--- a/solution.py
+++ b/solution.py
@@ -160,7 +160,10 @@
     incoming = passed_along(extended[tile_rows:], "base", 1)
     grid_tile = extended[:tile_rows].at[:KW].add(incoming)
     halves = row_transform(grid_tile, dft_table, tile_rows, channels_here)
-    columns = lax.all_to_all(halves, "base", split_axis=3, concat_axis=1, tiled=True)
+    columns = jnp.concatenate(
+        lax.all_to_all(jnp.stack(jnp.split(halves, lax.axis_size("base"), axis=3)), "base", 0, 0),
+        axis=1,
+    )
     stacked = to_columns(columns, tile_rows, channels_here)
     spectra = contract_slots(dft_table, stacked)
     normalizer = 1.0 / (channels_here * freq_count * slots * base_count)

time: 440 us -> 425 us (0.966)
  local copies, waits for them, and re-layouts: 55.1 us -> 42.1 us
    all_to_all x1 -> x0, local copies, waits for them, and re-layouts: 10.9 us -> none  [per_device(): lax.all_to_all(halves, 'base', split_axis=3, concat_axis=1, tiled=True)]
    another operation x4 -> x3, local copies, waits for them, and re-layouts: 14.2 us -> 6.96 us  [the longest x1 7.22 us: row_transform(): jnp.stack([jnp.dot(flat_rows, dft_table[:, :G], precision=HIGHEST_PRECISI...]
    reshape x0 -> x1, local copies, waits for them, and re-layouts: none -> 5.21 us  [per_device(): jnp.concatenate(lax.all_to_all(jnp.stack(jnp.split(halves, lax.axis_size(...]
    unnamed x61 -> x63, local copies, waits for them, and re-layouts: 11.4 us -> 11.4 us
where the time goes in v1:
time: 425 us; the launch traced here: 417 us
  blocking collectives  135 us (32%)
  matrix products  109 us (26%)
  other arithmetic  70.9 us (17%)
  local copies, waits for them, and re-layouts  42.1 us (10%)
  waiting for transfers between devices  35 us (8%)
  between operations  14.9 us (4%)
  starting transfers between devices  10.3 us (2%)
    all_to_all x1, blocking collectives, per_device(): lax.all_to_all(jnp.stack(jnp.split(halves, lax.axis_size('base'), axis=3)...  95.7 us
    dot_general x3, matrix products, contract_slots(): lax.dot_general(upper, lower, (((0,), (0,)), ((), ())), precision=HIGHEST...  53.6 us
    psum x1, blocking collectives, per_device(): lax.psum((bin_sums_local[0], bin_sums_local[1]), ('freq', 'base'))  39.3 us
    reduce_scatter x1, waiting for transfers between devices, per_device(): lax.psum_scatter(power_part, 'freq', scatter_dimension=0, tiled=True)  35 us
    dot_general x2, matrix products, add_block(): jnp.dot(values, onehot, precision=HIGHEST_PRECISION)  20.6 us
    sin x1, other arithmetic, dft_matrix(): sine = jnp.sin(angle)  17.6 us
    dot_general x1, matrix products, row_transform(): jnp.dot(flat_rows, dft_table[:, G:], precision=HIGHEST_PRECISION)  16.9 us
    dot_general x1, matrix products, row_transform(): jnp.dot(flat_rows, dft_table[:, :G], precision=HIGHEST_PRECISION)  16.5 us
  transfers between devices with their start and end apart: 3, of which 1 were waited for; matrix products, arithmetic and copies ran while one was open for 12% of the time, Pallas kernels for 0%

profile of v1, /device:TPU:0, one launch (start us, length us, event | category | flops | bytes accessed | tf_op | source)
XLA Modules:
  0.0 417.5 jit_solution(17929528038494484764)
XLA Ops:
  7.2 0.8 iota_compare_fusion.8
  8.0 0.7 broadcast_compare_fusion
  8.7 0.7 copy.132
  9.4 0.7 fusion.156
  10.1 2.4 reduce-window.6
  13.3 0.8 subtract_convert_fusion
  14.1 0.7 fusion.184
  14.8 1.6 convolution_bitcast_fusion
  16.4 0.7 convert_element_type.75
  17.1 0.7 compare_select_fusion.2
  18.3 1.8 scatter_custom_fusion
  20.5 1.8 scatter_custom_fusion.1
  22.6 0.8 copy.62
  23.4 6.3 %all-to-all-start = ((f32[4,2,20,256]{3,1,2,0:T(2,128)}), f32[4,2,20,256]{3,1,2,0:T(2,128)S(1)}, u32[]{:S(2)}, u32[]{:S(2)}) async-start(f32[4,2,20,256]{3,1,2,0:T(2,128)} %copy.62), calls=%async_computation | async-start | bytes 327680 | tf_op jit(solution)/shard_map/all_to_all | solution.py:150
  29.7 17.6 %fusion.36 = (f32[1024,1024]{1,0:T(8,128)}, f32[1024,1024]{1,0:T(8,128)}) fusion(), kind=kLoop, calls=%fused_computation.65 | loop fusion | flops 14680064 | bytes 8388608 | tf_op jit(solution)/shard_map/sin | solution.py:84
  47.3 16.5 %fusion.38 = f32[1024,1024]{1,0:T(8,128)} fusion(), kind=kLoop, calls=%fused_computation.67 | loop fusion | flops 15728640 | bytes 4194304 | tf_op jit(solution)/shard_map/neg | solution.py:86
  64.2 4.1 broadcast_multiply_fusion.1
  68.3 10.1 %fusion.9 = f32[264,2048]{1,0:T(8,128)} fusion(f32[1024,1024]{1,0:T(8,128)S(1)} %get-tuple-element.131, f32[1024,1024]{1,0:T(8,128)S(1)} %get-tuple-element.130, f32[1024]{0:T(1024)S(1)} %bitcast.287, f32[1024]{0:T(1024)S(1)} %bitcast.285, f32[1024]{0:T(1024)S(1)} %bitcast.283, f32[1024]{0:T(1024)S(1)} %bitcast.281, f32[1024]{0:T(1024)S(1)} %bitcast.279, ...), kind=kOutput, calls=%fused_computation.18 | convolution fusion | flops 6652362752 | bytes 10588160 | tf_op jit(solution)/shard_map/dot_general | solution.py:72
  78.4 3.2 stack_reshape.7
  81.8 4.1 broadcast_multiply_fusion.3
  86.0 10.1 %fusion.5 = f32[264,2048]{1,0:T(8,128)} fusion(f32[1024,1024]{1,0:T(8,128)S(1)} %get-tuple-element.133, f32[1024,1024]{1,0:T(8,128)S(1)} %get-tuple-element.132, f32[1024]{0:T(1024)S(1)} %bitcast.292, f32[1024]{0:T(1024)S(1)} %bitcast.290, f32[1024]{0:T(1024)S(1)} %bitcast.288, f32[1024]{0:T(1024)S(1)} %bitcast.286, f32[1024]{0:T(1024)S(1)} %bitcast.284, ...), kind=kOutput, calls=%fused_computation.14 | convolution fusion | flops 6652362752 | bytes 10588160 | tf_op jit(solution)/shard_map/dot_general | solution.py:72
  96.1 4.1 stack_reshape.6
  100.2 2.5 constant_dynamic-update-slice_fusion.1
  102.7 0.9 constant_dynamic-update-slice_fusion
  103.6 3.9 collective-permute-start
  107.5 12.8 %maximum_maximum_fusion = f32[2048,2048]{1,0:T(8,128)} fusion(f32[1024,1024]{1,0:T(8,128)S(1)} %copy-done.3, f32[1024,1024]{1,0:T(8,128)S(1)} %copy-done.1, f32[1024,1024]{1,0:T(8,128)} %fusion.38), kind=kLoop, calls=%fused_computation.9 | loop fusion | flops 12582912 | bytes 29360128 | tf_op jit(solution)/shard_map/concatenate | solution.py:85
  120.4 3.4 slice.363
  123.7 0.8 fusion.151
  124.5 6.7 %reshape.404 = f32[256,2,2048]{2,0,1:T(8,128)} reshape(f32[256,2,2,1024]{3,2,0,1:T(2,128)} %fusion.151) | data formatting | bytes 8388608 | tf_op jit(solution)/shard_map/reshape.291
  131.2 16.9 %fusion.40 = f32[1,256,2,1024]{3,1,2,0:T(8,128)S(1)} fusion(f32[256,2,2048]{2,0,1:T(8,128)} %reshape.404, f32[2048,2048]{1,0:T(8,128)} %maximum_maximum_fusion), kind=kOutput, calls=%fused_computation.69 | convolution fusion | flops 12884901888 | bytes 14680064 | tf_op jit(solution)/shard_map/dot_general | solution.py:95
  148.1 16.5 %fusion.39 = f32[1,256,2,1024]{3,1,2,0:T(8,128)S(1)} fusion(f32[256,2,2048]{2,0,1:T(8,128)S(1)} %copy-done.6, f32[2048,2048]{1,0:T(8,128)} %maximum_maximum_fusion), kind=kOutput, calls=%fused_computation.68 | convolution fusion | flops 12884901888 | bytes 14680064 | tf_op jit(solution)/shard_map/dot_general | solution.py:94
  164.6 0.5 fusion.106
  165.4 95.7 %all_to_all.10 = f32[4,2,256,2,256]{4,2,3,1,0:T(8,128)S(1)} all-to-all(f32[4,2,256,2,256]{4,2,3,1,0:T(8,128)S(1)} %pad_maximum_fusion), channel_id=1, replica_groups=mesh['freq'=8,'base'=4] {'base'}, dimensions={0} | all-to-all | bytes 8388608 | tf_op jit(solution)/shard_map/all_to_all | solution.py:164
  261.1 5.2 %copy.65 = f32[2,4,256,2,256]{4,3,2,1,0:T(2,128)} copy(f32[2,4,256,2,256]{4,2,3,0,1:T(8,128)S(1)} %bitcast.235) | data formatting | bytes 8388608 | tf_op jit(solution)/shard_map/reshape | solution.py:163
  266.4 4.9 %copy.116 = f32[256,8,2,256]{3,1,2,0:T(8,128)} copy(f32[256,8,2,256]{3,2,1,0:T(2,128)} %bitcast.236) | data formatting | bytes 8388608
  271.3 1.3 copy-done.4
  272.6 33.4 %fusion.182 = f32[2048,512]{0,1:T(8,128)} fusion(f32[2048,512]{1,0:T(8,128)} %bitcast.238, f32[1024,1024]{1,0:T(8,128)S(1)} %copy-done.4, f32[1024,1024]{1,0:T(8,128)S(1)} %copy-done.2, f32[1024,1024]{1,0:T(8,128)S(1)} %copy-done.5), kind=kOutput, calls=%fused_computation.271 | convolution fusion | flops 25782386688 | bytes 20971520 | tf_op jit(solution)/shard_map/dot_general | solution.py:72
  306.0 2.7 fusion.35
  308.7 1.2 reduce_sum.19
  309.9 2.3 broadcast_multiply_fusion.4
  312.5 35.0 %reduce-scatter.2.cloned.1.call-done = f32[128,256]{0,1:T(8,128)} async-done(((f32[1024,256]{0,1:T(8,128)}), f32[128,256]{0,1:T(8,128)}) %reduce-scatter.2.cloned.1.call-update) | async-done | bytes 131088 | tf_op jit(solution)/shard_map/reduce_scatter | solution.py:175
  347.5 1.0 copy.75
  348.8 21.1 %while.12 = (s32[]{:T(128)}, f32[2,512]{1,0:T(2,128)S(1)}, f32[2,2,16384]{2,0,1:T(2,128)S(1)}, s32[2,16384]{1,0:T(2,128)S(1)}, s32[]{:T(128)}, /*index=5*/s32[]{:T(128)}) while((s32[]{:T(128)}, f32[2,512]{1,0:T(2,128)S(1)}, f32[2,2,16384]{2,0,1:T(2,128)S(1)}, s32[2,16384]{1,0:T(2,128)S(1)}, s32[]{:T(128)}, ...), condition=%wide.region_8.9_spmd.clone, body=%wide.region_7.8_spmd.clone.sunk | while | flops 209717248 | bytes 598103 | solution.py:120
  349.0 10.3 %fusion.190 = f32[2,512]{1,0:T(2,128)S(1)} fusion(s32[16384]{0:T(1024)S(1)} %bitcast.242, f32[1,2,16384]{2,0,1:T(1,128)S(1)} %constant_dynamic-slice_fusion.5, f32[2,512]{1,0:T(2,128)S(1)} %get-tuple-element.180, pred[]{:T(512)S(6)} %compare.11), kind=kOutput, calls=%fused_computation.5.clone.1 | convolution fusion | flops 209717248 | bytes 204801 | tf_op jit(solution)/shard_map/while/body/eval_jaxpr/dot_general | solution.py:118
  359.5 10.3 %fusion.190 = f32[2,512]{1,0:T(2,128)S(1)} fusion(s32[16384]{0:T(1024)S(1)} %bitcast.242, f32[1,2,16384]{2,0,1:T(1,128)S(1)} %constant_dynamic-slice_fusion.5, f32[2,512]{1,0:T(2,128)S(1)} %get-tuple-element.180, pred[]{:T(512)S(6)} %compare.11), kind=kOutput, calls=%fused_computation.5.clone.1 | convolution fusion | flops 209717248 | bytes 204801 | tf_op jit(solution)/shard_map/while/body/eval_jaxpr/dot_general | solution.py:118
  369.9 39.3 %all-reduce.1 = (f32[512]{0:T(512)S(1)}, f32[512]{0:T(512)S(1)}) all-reduce(f32[512]{0:T(512)S(1)} %bitcast.272, f32[512]{0:T(512)S(1)} %bitcast.271), channel_id=1, replica_groups=mesh['freq'=8,'base'=4] {'freq','base'}, use_global_device_ids=true, to_apply=%region_9.10 | all-reduce | flops 1024 | bytes 8192 | tf_op jit(solution)/shard_map/psum | solution.py:178
  409.1 0.6 div.3
  409.7 0.8 copy.69
  (95 shorter events, 3.4 us)
Async XLA Ops:
  7.2 305.1 %copy-start = (s32[256,1024]{1,0:T(8,128)S(1)}, s32[256,1024]{1,0:T(8,128)}, u32[]{:S(2)}) copy-start(s32[256,1024]{1,0:T(8,128)} %param.19) | copy-start | bytes 3145732
  23.4 40.4 %all-to-all-start = ((f32[4,2,20,256]{3,1,2,0:T(2,128)}), f32[4,2,20,256]{3,1,2,0:T(2,128)S(1)}, u32[]{:S(2)}, u32[]{:S(2)}) async-start(f32[4,2,20,256]{3,1,2,0:T(2,128)} %copy.62), calls=%async_computation | async-start | bytes 327680 | tf_op jit(solution)/shard_map/all_to_all | solution.py:150
  29.7 317.8 %reduce-scatter.2.cloned.1.call-start = ((), (), s32[]{:S(2)}) async-start(), calls=%async_computation.3 | async-start | bytes 1179648 | tf_op jit(solution)/shard_map/reduce_scatter | solution.py:175
  100.2 7.4 %copy-start.1 = (f32[1024,1024]{1,0:T(8,128)S(1)}, f32[1024,1024]{1,0:T(8,128)}, u32[]{:S(2)}) copy-start(f32[1024,1024]{1,0:T(8,128)} %get-tuple-element.146) | copy-start | bytes 12582916
  100.2 7.4 %copy-start.3 = (f32[1024,1024]{1,0:T(8,128)S(1)}, f32[1024,1024]{1,0:T(8,128)}, u32[]{:S(2)}) copy-start(f32[1024,1024]{1,0:T(8,128)} %get-tuple-element.147) | copy-start | bytes 12582916
  103.6 20.2 %collective-permute-start = (f32[8,2,2,1024]{3,2,0,1:T(2,128)S(1)}, f32[8,2,2,1024]{3,2,0,1:T(2,128)S(1)}, u32[]{:S(2)}, u32[]{:S(2)}) collective-permute-start(f32[8,2,2,1024]{3,2,0,1:T(2,128)S(1)} %slice.365), channel_id=1, source_target_pairs={{0,1},{1,2},{2,3},{4,5},{5,6},{6,7},{8,9},{9,10},{10,11},{12,13},{... | collective-permute-start | bytes 393224 | tf_op jit(solution)/shard_map/ppermute | solution.py:16
  131.2 16.9 %copy-start.6 = (f32[256,2,2048]{2,0,1:T(8,128)S(1)}, f32[256,2,2048]{2,0,1:T(8,128)}, u32[]{:S(2)}) copy-start(f32[256,2,2048]{2,0,1:T(8,128)} %reshape.404) | copy-start | bytes 12582916
  261.1 10.2 %copy-start.5 = (f32[1024,1024]{1,0:T(8,128)S(1)}, f32[1024,1024]{1,0:T(8,128)}, u32[]{:S(2)}) copy-start(f32[1024,1024]{1,0:T(8,128)} %fusion.38) | copy-start | bytes 12582916
  266.3 4.9 %copy-start.2 = (f32[1024,1024]{1,0:T(8,128)S(1)}, f32[1024,1024]{1,0:T(8,128)}, u32[]{:S(2)}) copy-start(f32[1024,1024]{1,0:T(8,128)} %get-tuple-element.146) | copy-start | bytes 12582916
  266.4 6.2 %copy-start.4 = (f32[1024,1024]{1,0:T(8,128)S(1)}, f32[1024,1024]{1,0:T(8,128)}, u32[]{:S(2)}) copy-start(f32[1024,1024]{1,0:T(8,128)} %get-tuple-element.147) | copy-start | bytes 12582916
  348.8 61.0 %copy-start.7 = (f32[128,256]{0,1:T(8,128)S(1)}, f32[128,256]{0,1:T(8,128)}, u32[]{:S(2)}) copy-start(f32[128,256]{0,1:T(8,128)} %reduce-scatter.2.cloned.1.call-done) | copy-start | bytes 393220
Sparse Core Ops, SparseCore 0:
  312.4 35.1 reduce-scatter.1
